TPU v7x, 32 devices: a whole 2x2x4 slice. The times are simulated.
32 devices in a mesh: pipe: 8 (over z, y), tensor: 4 (over x, core).
Axes of the slice: x: 2, y: 2, z: 4, core: 2. Of those that a mesh axis runs over, the one named last changes fastest.
Arguments:
- memory: bfloat16 [2, 512, 4096], P(None, 'pipe', 'tensor'), may hold values from -6 to 6
- states: bfloat16 [8, 2, 256, 4096], P('pipe', None, None, 'tensor'), may hold values from -6 to 6
- norm_gain: float32 [8, 4096], P('pipe'), may hold values from 0.25 to 1.75
- w_query: bfloat16 [8, 4096, 4096], P('pipe', None, 'tensor'), may hold values from -0.09375 to 0.09375
- w_keyvalue: bfloat16 [8, 4096, 2, 4096], P('pipe', None, None, 'tensor'), may hold values from -0.09375 to 0.09375
- w_output: bfloat16 [8, 4096, 4096], P('pipe', 'tensor'), may hold values from -0.125 to 0.125
Outputs:
- updated: bfloat16 [8, 2, 256, 4096], P('pipe', None, None, 'tensor')
All inputs are finite; a program needn't handle non-finite values.
Results may differ from a plain program's by a relative error of at most 0.006.
Values may be sent and summed in bfloat16 or wider, within the bound.
A program may use at most 128 MiB of HBM per device.

v0:
```python
import jax
import jax.numpy as jnp
from jax import lax
from jax.sharding import PartitionSpec as P

HEAD_DIM = 64


def per_device(memory, states, norm_gain, w_query, w_keyvalue, w_output):
    whole_states = lax.all_gather(states[0], "tensor", axis=2, tiled=True)
    xf = whole_states.astype(jnp.float32)
    scale = lax.rsqrt(jnp.mean(xf * xf, axis=-1, keepdims=True) + 1e-06)
    normed = (xf * scale * norm_gain[0]).astype(jnp.bfloat16)
    weight_q = w_query[0]
    local_inner = weight_q.shape[1]
    weight_kv = w_keyvalue[0].reshape(w_keyvalue.shape[1], 2 * local_inner)
    weight_o = w_output[0]
    seqs = normed.shape[0]
    dec_rows = normed.shape[1]
    local_heads = local_inner // HEAD_DIM
    query = jnp.einsum("btd,de->bte", normed, weight_q, preferred_element_type=jnp.float32).astype(
        jnp.bfloat16
    )
    gathered = lax.all_gather(memory, "pipe", axis=1, tiled=True)
    gathered = lax.all_gather(gathered, "tensor", axis=2, tiled=True)
    keyvalue = jnp.einsum(
        "bpd,de->bpe", gathered, weight_kv, preferred_element_type=jnp.float32
    ).astype(jnp.bfloat16)
    enc_rows = keyvalue.shape[1]
    keys = keyvalue[:, :, :local_inner].reshape(seqs, enc_rows, local_heads, HEAD_DIM)
    values = keyvalue[:, :, local_inner:].reshape(seqs, enc_rows, local_heads, HEAD_DIM)
    heads_q = query.reshape(seqs, dec_rows, local_heads, HEAD_DIM)
    scores = jnp.einsum(
        "bqhd,bkhd->bhqk", heads_q, keys, preferred_element_type=jnp.float32
    ) / jnp.sqrt(jnp.float32(HEAD_DIM))
    probs = jax.nn.softmax(scores, axis=-1).astype(jnp.bfloat16)
    context = jnp.einsum(
        "bhqk,bkhd->bqhd", probs, values, preferred_element_type=jnp.float32
    ).astype(jnp.bfloat16)
    context = context.reshape(seqs, dec_rows, local_inner)
    partial_terms = jnp.einsum("bte,ed->btd", context, weight_o, preferred_element_type=jnp.float32)
    branch = lax.psum_scatter(partial_terms, "tensor", scatter_dimension=2, tiled=True)
    result = (states[0].astype(jnp.float32) + branch).astype(jnp.bfloat16)
    return result[None]


def solution(mesh):
    in_specs = (
        P(None, "pipe", "tensor"),
        P("pipe", None, None, "tensor"),
        P("pipe", None),
        P("pipe", None, "tensor"),
        P("pipe", None, None, "tensor"),
        P("pipe", "tensor", None),
    )
    out_specs = P("pipe", None, None, "tensor")
    return jax.shard_map(
        per_device, mesh=mesh, in_specs=in_specs, out_specs=out_specs, check_vma=False
    )
```

profile of v0, /device:TPU:0, one launch (start us, length us, event | category | flops | bytes accessed | tf_op | source)
XLA Modules:
  0.0 294.8 jit_solution(15955444793238928033)
XLA Ops:
  6.5 0.0 all-gather.5.cloned.1.call-start
  6.5 0.7 all-gather.5.cloned.1.call-update
  7.3 0.0 all-gather.9.cloned.1.call-start
  7.3 0.7 all-gather.9.cloned.1.call-update
  8.0 0.0 all-gather.7.cloned.1.call-start
  8.1 53.3 %all-gather.5.cloned.1.call-done = bf16[2,512,1024]{2,1,0:T(8,128)(2,1)} async-done(((bf16[2,64,1024]{2,1,0:T(8,128)(2,1)}), bf16[2,512,1024]{2,1,0:T(8,128)(2,1)}) %all-gather.5.cloned.1.call-update) | async-done | bytes 2097168 | tf_op jit(solution)/shard_map/all_gather | solution.py:24
  61.3 0.0 all-gather.7.cloned.1.call-update
  61.4 0.0 reduce-scatter.2.cloned.1.call-start
  61.4 28.0 %reshape.30 = bf16[4096,2048,1]{1,0,2:T(8,128)(2,1)} reshape(bf16[1,4096,2,1024]{3,2,1,0:T(2,128)(2,1)} %param.10) | data formatting | bytes 33554432 | tf_op jit(solution)/shard_map/reshape;squeeze | solution.py:16
  89.4 6.5 %all-gather.9.cloned.1.call-done = bf16[1,2,256,4096]{3,2,1,0:T(8,128)(2,1)} async-done(((bf16[1,2,256,1024]{3,2,1,0:T(8,128)(2,1)}), bf16[1,2,256,4096]{3,2,1,0:T(8,128)(2,1)}) %all-gather.9.cloned.1.call-update) | async-done | bytes 4194320 | tf_op jit(solution)/shard_map/all_gather | solution.py:10
  95.9 3.1 %fusion.4 = f32[2,256]{1,0:T(2,128)S(1)} fusion(bf16[1,2,256,4096]{3,2,1,0:T(8,128)(2,1)} %all-gather.9.cloned.1.call-done), kind=kLoop, calls=%fused_computation.7 | loop fusion | flops 6290944 | bytes 4196352 | tf_op jit(solution)/shard_map/reduce_sum | solution.py:12
  99.0 9.3 %fusion.21 = bf16[2,256,1024]{2,1,0:T(8,128)(2,1)S(1)} fusion(bf16[1,4096,1024]{2,1,0:T(8,128)(2,1)} %param.9, bf16[1,2,256,4096]{3,2,1,0:T(8,128)(2,1)} %all-gather.9.cloned.1.call-done, f32[4096]{0:T(1024)S(1)} %bitcast.43, f32[2,256]{1,0:T(2,128)S(1)} %add_rsqrt_fusion), kind=kOutput, calls=%fused_computation.24 | convolution fusion | flops 4303880192 | bytes 13649920 | tf_op jit(solution)/shard_map/btd,de->bte/dot_general | solution.py:21
  108.4 0.5 copy.12
  108.9 46.9 %all-gather.7.cloned.1.call-done = bf16[2,512,4096]{2,1,0:T(8,128)(2,1)} async-done(((bf16[2,512,1024]{2,1,0:T(8,128)(2,1)}), bf16[2,512,4096]{2,1,0:T(8,128)(2,1)}) %all-gather.7.cloned.1.call-update) | async-done | bytes 8388624 | tf_op jit(solution)/shard_map/all_gather | solution.py:25
  155.8 22.7 %convolution_convert_fusion = bf16[2,512,2048]{2,1,0:T(8,128)(2,1)S(1)} fusion(bf16[2,512,4096]{2,1,0:T(8,128)(2,1)} %all-gather.7.cloned.1.call-done, bf16[4096,2048,1]{1,0,2:T(8,128)(2,1)} %reshape.30), kind=kOutput, calls=%fused_computation.19 | convolution fusion | flops 17181966336 | bytes 29360128 | tf_op jit(solution)/shard_map/bpd,de->bpe/dot_general | solution.py:26
  178.5 1.8 fusion.28
  180.3 3.9 %copy.11 = bf16[2,512,1024]{1,2,0:T(8,128)(2,1)} copy(bf16[2,512,1024]{2,1,0:T(8,128)(2,1)} %get-tuple-element.6) | data formatting | bytes 4194304 | tf_op jit(solution)/shard_map/slice | solution.py:31
  184.2 2.5 copy.13
  186.7 9.7 %fusion.29 = (f32[2,16,256]{2,1,0:T(8,128)S(1)}, f32[2,16,256,512]{3,2,1,0:T(8,128)}) fusion(bf16[2,256,16,64]{1,3,2,0:T(8,128)(2,1)S(1)} %bitcast.42, bf16[2,512,16,64]{1,3,2,0:T(8,128)(2,1)} %bitcast.40), kind=kOutput, calls=%fused_computation.29 | convolution fusion | flops 549454336 | bytes 19955712 | tf_op jit(solution)/shard_map/sub | solution.py:36
  196.5 7.3 %fusion.20 = bf16[2,16,64,256]{3,2,1,0:T(8,128)(2,1)S(1)} fusion(bf16[2,512,16,64]{1,3,2,0:T(8,128)(2,1)S(1)} %bitcast.39, f32[2,16,256,512]{3,2,1,0:T(8,128)} %get-tuple-element.8, f32[2,16,256]{2,1,0:T(8,128)S(1)} %get-tuple-element.7), kind=kOutput, calls=%fused_computation.23 | convolution fusion | flops 545783808 | bytes 19955712 | tf_op jit(solution)/shard_map/bhqk,bkhd->bqhd/dot_general | solution.py:37
  203.8 10.2 %fusion.7 = f32[2,256,4096]{2,1,0:T(8,128)} fusion(bf16[2,256,1024]{1,2,0:T(8,128)(2,1)S(1)} %bitcast.41, bf16[1,1024,4096]{2,1,0:T(8,128)(2,1)} %param.11), kind=kOutput, calls=%fused_computation.10 | convolution fusion | flops 4294967296 | bytes 17825792 | tf_op jit(solution)/shard_map/bte,ed->btd/dot_general | solution.py:41
  213.9 0.0 reduce-scatter.2.cloned.1.call-update
  214.0 71.4 %reduce-scatter.2.cloned.1.call-done = f32[2,256,1024]{2,1,0:T(8,128)} async-done(((f32[2,256,4096]{2,1,0:T(8,128)}), f32[2,256,1024]{2,1,0:T(8,128)}) %reduce-scatter.2.cloned.1.call-update) | async-done | bytes 2097168 | tf_op jit(solution)/shard_map/reduce_scatter | solution.py:42
  285.4 2.9 fusion.26
  (7 shorter events, 0.0 us)
Async XLA Ops:
  6.5 54.8 %all-gather.5.cloned.1.call-start = ((), (), s32[]{:S(2)}) async-start(), calls=%async_computation.1 | async-start | bytes 2359296 | tf_op jit(solution)/shard_map/all_gather | solution.py:24
  7.3 88.7 %all-gather.9.cloned.1.call-start = ((), (), s32[]{:S(2)}) async-start(), calls=%async_computation.4 | async-start | bytes 5242880 | tf_op jit(solution)/shard_map/all_gather | solution.py:10
  8.0 147.8 %all-gather.7.cloned.1.call-start = ((), (), s32[]{:S(2)}) async-start(), calls=%async_computation.2 | async-start | bytes 10485760 | tf_op jit(solution)/shard_map/all_gather | solution.py:25
  61.4 37.7 %copy-start.2 = (f32[1,4096]{1,0:T(1,128)S(1)}, f32[1,4096]{1,0:T(1,128)}, u32[]{:S(2)}) copy-start(f32[1,4096]{1,0:T(1,128)} %param.8) | copy-start | bytes 49156
  61.4 224.0 %reduce-scatter.2.cloned.1.call-start = ((), (), s32[]{:S(2)}) async-start(), calls=%async_computation.3 | async-start | bytes 10485760 | tf_op jit(solution)/shard_map/reduce_scatter | solution.py:42
  186.7 9.8 %copy-start.1 = (bf16[2,512,1024]{1,2,0:T(8,128)(2,1)S(1)}, bf16[2,512,1024]{1,2,0:T(8,128)(2,1)}, u32[]{:S(2)}) copy-start(bf16[2,512,1024]{1,2,0:T(8,128)(2,1)} %copy.11) | copy-start | bytes 6291460
  213.9 71.4 %copy-start = (bf16[1,2,256,1024]{3,2,1,0:T(8,128)(2,1)S(1)}, bf16[1,2,256,1024]{3,2,1,0:T(8,128)(2,1)}, u32[]{:S(2)}) copy-start(bf16[1,2,256,1024]{3,2,1,0:T(8,128)(2,1)} %param.7) | copy-start | bytes 3145732
Sparse Core Ops, SparseCore 0:
  9.5 51.7 all-gather.4
  62.9 32.9 all-gather.8
  97.5 58.2 all-gather.6
  214.1 71.2 reduce-scatter.1
where the time goes:
time: 296 us; the launch traced here: 295 us
  waiting for transfers between devices  180 us (61%)
  matrix products  59.2 us (20%)
  local copies, waits for them, and re-layouts  36.7 us (12%)
  between operations  13.2 us (4%)
  other arithmetic  6 us (2%)
    reduce_scatter x1, waiting for transfers between devices, per_device(): lax.psum_scatter(partial_terms, 'tensor', scatter_dimension=2, tiled=True)  71.4 us
    all_gather x1, waiting for transfers between devices, per_device(): gathered = lax.all_gather(memory, 'pipe', axis=1, tiled=True)  53.3 us
    all_gather x1, waiting for transfers between devices, per_device(): gathered = lax.all_gather(gathered, 'tensor', axis=2, tiled=True)  46.9 us
    another operation x1, local copies, waits for them, and re-layouts, per_device(): weight_kv = w_keyvalue[0].reshape(w_keyvalue.shape[1], 2 * local_inner)  28 us
    dot_general x1, matrix products, per_device(): jnp.einsum('bpd,de->bpe', gathered, weight_kv, preferred_element_type=jnp...  22.7 us
    dot_general x1, matrix products, per_device(): jnp.einsum('bte,ed->btd', context, weight_o, preferred_element_type=jnp.f...  10.2 us
    sub x1, matrix products, per_device(): probs = jax.nn.softmax(scores, axis=-1).astype(jnp.bfloat16)  9.75 us
    dot_general x1, matrix products, per_device(): jnp.einsum('btd,de->bte', normed, weight_q, preferred_element_type=jnp.fl...  9.34 us
  transfers between devices with their start and end apart: 4, of which 4 were waited for; matrix products, arithmetic and copies ran while one was open for 14% of the time, Pallas kernels for 0%

commit v1 on v0

--- a/solution.py
+++ b/solution.py
@@ -22,7 +22,14 @@
         jnp.bfloat16
     )
     gathered = lax.all_gather(memory, "pipe", axis=1, tiled=True)
-    gathered = lax.all_gather(gathered, "tensor", axis=2, tiled=True)
+    size = lax.axis_size("tensor")
+    forward = [(i, (i + 1) % size) for i in range(size)]
+    parts = [gathered]
+    for far in range(1, size):
+        parts = [lax.ppermute(parts[0], "tensor", forward), *parts]
+    whole = jnp.concatenate(parts, axis=2)
+    shift = (lax.axis_index("tensor") + 1) * parts[-1].shape[2]
+    gathered = jnp.roll(whole, shift, axis=2)
     keyvalue = jnp.einsum(
         "bpd,de->bpe", gathered, weight_kv, preferred_element_type=jnp.float32
     ).astype(jnp.bfloat16)

time: 296 us -> 334 us (1.13)
  local copies, waits for them, and re-layouts: 36.7 us -> 58.4 us
  waiting for transfers between devices: 180 us -> 199 us
    ppermute x0 -> x3, waiting for transfers between devices: none -> 73.7 us  [per_device(): parts = [lax.ppermute(parts[0], 'tensor', forward), *parts]]
    all_gather x1 -> x0, waiting for transfers between devices: 46.9 us -> none  [per_device(): gathered = lax.all_gather(gathered, 'tensor', axis=2, tiled=True)]
    unnamed x6 -> x27, local copies, waits for them, and re-layouts: 0.01 us -> 19.2 us
    all_gather x1, waiting for transfers between devices: 6.53 us -> 0.01 us  [per_device(): whole_states = lax.all_gather(states[0], 'tensor', axis=2, tiled=True)]
  transfers between devices with their start and end apart: 4 -> 6, of which waited for: 4 -> 4; matrix products, arithmetic and copies ran while one was open for 14% -> 13% of each run, Pallas kernels for 0% -> 0%
where the time goes in v1:
time: 334 us; the launch traced here: 333 us
  waiting for transfers between devices  199 us (60%)
  local copies, waits for them, and re-layouts  58.4 us (17%)
  matrix products  57 us (17%)
  between operations  13.2 us (4%)
  other arithmetic  6.01 us (2%)
    ppermute x3, waiting for transfers between devices, per_device(): parts = [lax.ppermute(parts[0], 'tensor', forward), *parts]  73.7 us
    reduce_scatter x1, waiting for transfers between devices, per_device(): lax.psum_scatter(partial_terms, 'tensor', scatter_dimension=2, tiled=True)  70.3 us
    all_gather x1, waiting for transfers between devices, per_device(): gathered = lax.all_gather(memory, 'pipe', axis=1, tiled=True)  53.3 us
    another operation x1, local copies, waits for them, and re-layouts, per_device(): weight_kv = w_keyvalue[0].reshape(w_keyvalue.shape[1], 2 * local_inner)  27.7 us
    dot_general x1, matrix products, per_device(): jnp.einsum('bpd,de->bpe', gathered, weight_kv, preferred_element_type=jnp...  19.6 us
    unnamed x27, local copies, waits for them, and re-layouts  19.2 us
    dot_general x1, matrix products, per_device(): jnp.einsum('bte,ed->btd', context, weight_o, preferred_element_type=jnp.f...  10.2 us
    dot_general x1, matrix products, per_device(): jnp.einsum('btd,de->bte', normed, weight_q, preferred_element_type=jnp.fl...  10.2 us
  transfers between devices with their start and end apart: 6, of which 4 were waited for; matrix products, arithmetic and copies ran while one was open for 13% of the time, Pallas kernels for 0%

profile of v1, /device:TPU:0, one launch (start us, length us, event | category | flops | bytes accessed | tf_op | source)
XLA Modules:
  0.0 333.4 jit_solution(17153845093152811667)
XLA Ops:
  8.1 53.3 %all-gather.4.cloned.1.call-done = bf16[2,512,1024]{2,1,0:T(8,128)(2,1)} async-done(((bf16[2,64,1024]{2,1,0:T(8,128)(2,1)}), bf16[2,512,1024]{2,1,0:T(8,128)(2,1)}) %all-gather.4.cloned.1.call-update) | async-done | bytes 2097168 | tf_op jit(solution)/shard_map/all_gather | solution.py:24
  61.3 48.1 %collective-permute-done = bf16[2,512,1024]{2,1,0:T(8,128)(2,1)S(1)} collective-permute-done((bf16[2,512,1024]{2,1,0:T(8,128)(2,1)}, bf16[2,512,1024]{2,1,0:T(8,128)(2,1)S(1)}, u32[]{:S(2)}, u32[]{:S(2)}) %collective-permute-start) | collective-permute-done | bytes 2097184 | tf_op jit(solution)/shard_map/ppermute | solution.py:29
  110.8 25.6 %collective-permute-done.1 = bf16[2,512,1024]{2,1,0:T(8,128)(2,1)} collective-permute-done((bf16[2,512,1024]{2,1,0:T(8,128)(2,1)S(1)}, bf16[2,512,1024]{2,1,0:T(8,128)(2,1)}, u32[]{:S(2)}, u32[]{:S(2)}) %collective-permute-start.1) | collective-permute-done | bytes 2097184 | tf_op jit(solution)/shard_map/ppermute | solution.py:29
  136.4 27.7 %reshape.30 = bf16[4096,2048,1]{1,0,2:T(8,128)(2,1)} reshape(bf16[1,4096,2,1024]{3,2,1,0:T(2,128)(2,1)} %param.10) | data formatting | bytes 33554432 | tf_op jit(solution)/shard_map/reshape;squeeze | solution.py:16
  164.1 3.1 fusion.4
  167.2 10.2 %fusion.26 = bf16[2,256,1024]{2,1,0:T(8,128)(2,1)} fusion(bf16[1,4096,1024]{2,1,0:T(8,128)(2,1)} %param.9, bf16[1,2,256,4096]{3,2,1,0:T(8,128)(2,1)} %all-gather.6.cloned.1.call-done, f32[4096]{0:T(1024)S(1)} %bitcast.44, f32[2,256]{1,0:T(2,128)S(1)} %add_rsqrt_fusion), kind=kOutput, calls=%fused_computation.26 | convolution fusion | flops 4303880192 | bytes 13649920 | tf_op jit(solution)/shard_map/btd,de->bte/dot_general | solution.py:21
  177.4 1.6 copy.12
  179.0 3.3 constant_dynamic-update-slice_fusion.7
  182.3 3.1 constant_dynamic-update-slice_fusion.6
  185.4 1.5 constant_dynamic-update-slice_fusion.5
  186.9 1.5 constant_dynamic-update-slice_fusion.4
  188.4 3.2 constant_dynamic-update-slice_fusion.3
  191.6 3.1 constant_dynamic-update-slice_fusion.2
  194.7 1.5 constant_dynamic-update-slice_fusion.1
  196.2 1.5 constant_dynamic-update-slice_fusion
  198.4 19.6 %fusion.19 = bf16[2,512,2048]{2,1,0:T(8,128)(2,1)S(1)} fusion(bf16[4096,2048,1]{1,0,2:T(8,128)(2,1)S(1)} %bitcast.39, bf16[2,512,8192]{2,1,0:T(8,128)(2,1)} %constant_dynamic-update-slice_fusion, s32[]{:T(128)S(6)} %select_n.14), kind=kOutput, calls=%fused_computation.21 | convolution fusion | flops 17181966336 | bytes 29360132 | tf_op jit(solution)/shard_map/bpd,de->bpe/dot_general | solution.py:33
  218.0 1.9 fusion.34
  219.8 3.9 %copy.13 = bf16[2,512,1024]{1,2,0:T(8,128)(2,1)} copy(bf16[2,512,1024]{2,1,0:T(8,128)(2,1)} %get-tuple-element.5) | data formatting | bytes 4194304 | tf_op jit(solution)/shard_map/slice | solution.py:37
  223.8 2.6 copy.11
  226.4 9.8 %fusion.35 = (f32[2,16,256]{2,1,0:T(8,128)S(1)}, f32[2,16,256,512]{3,2,1,0:T(8,128)}) fusion(bf16[2,256,16,64]{1,3,2,0:T(8,128)(2,1)S(1)} %bitcast.43, bf16[2,512,16,64]{1,3,2,0:T(8,128)(2,1)} %bitcast.40), kind=kOutput, calls=%fused_computation.40 | convolution fusion | flops 549454336 | bytes 19955712 | tf_op jit(solution)/shard_map/sub | solution.py:43
  236.2 7.3 %fusion.25 = bf16[2,16,64,256]{3,2,1,0:T(8,128)(2,1)S(1)} fusion(bf16[2,512,16,64]{1,3,2,0:T(8,128)(2,1)S(1)} %bitcast.41, f32[2,16,256,512]{3,2,1,0:T(8,128)} %get-tuple-element.8, f32[2,16,256]{2,1,0:T(8,128)S(1)} %get-tuple-element.7), kind=kOutput, calls=%fused_computation.25 | convolution fusion | flops 545783808 | bytes 19955712 | tf_op jit(solution)/shard_map/bhqk,bkhd->bqhd/dot_general | solution.py:44
  243.4 10.2 %fusion.7 = f32[2,256,4096]{2,1,0:T(8,128)} fusion(bf16[2,256,1024]{1,2,0:T(8,128)(2,1)S(1)} %bitcast.42, bf16[1,1024,4096]{2,1,0:T(8,128)(2,1)} %param.11), kind=kOutput, calls=%fused_computation.10 | convolution fusion | flops 4294967296 | bytes 17825792 | tf_op jit(solution)/shard_map/bte,ed->btd/dot_general | solution.py:48
  253.7 70.3 %reduce-scatter.2.cloned.1.call-done = f32[2,256,1024]{2,1,0:T(8,128)} async-done(((f32[2,256,4096]{2,1,0:T(8,128)}), f32[2,256,1024]{2,1,0:T(8,128)}) %reduce-scatter.2.cloned.1.call-update) | async-done | bytes 2097168 | tf_op jit(solution)/shard_map/reduce_scatter | solution.py:49
  323.9 2.9 fusion.31
  (33 shorter events, 3.5 us)
Async XLA Ops:
  6.5 54.8 %all-gather.4.cloned.1.call-start = ((), (), s32[]{:S(2)}) async-start(), calls=%async_computation.1 | async-start | bytes 2359296 | tf_op jit(solution)/shard_map/all_gather | solution.py:24
  7.3 156.8 %all-gather.6.cloned.1.call-start = ((), (), s32[]{:S(2)}) async-start(), calls=%async_computation.3 | async-start | bytes 5242880 | tf_op jit(solution)/shard_map/all_gather | solution.py:10
  8.0 315.9 %reduce-scatter.2.cloned.1.call-start = ((), (), s32[]{:S(2)}) async-start(), calls=%async_computation.2 | async-start | bytes 10485760 | tf_op jit(solution)/shard_map/reduce_scatter | solution.py:49
  61.3 48.1 %collective-permute-start = (bf16[2,512,1024]{2,1,0:T(8,128)(2,1)}, bf16[2,512,1024]{2,1,0:T(8,128)(2,1)S(1)}, u32[]{:S(2)}, u32[]{:S(2)}) collective-permute-start(bf16[2,512,1024]{2,1,0:T(8,128)(2,1)} %all-gather.4.cloned.1.call-done), channel_id=1, source_target_pairs={{0,1},{1,2},{2,3},{3,0},{4,5},{5,6},{6,7},{7,4},{8,9},{9,10},{10,1... | collective-permute-start | bytes 6291464 | tf_op jit(solution)/shard_map/ppermute | solution.py:29
  109.5 1.3 copy-start.1
  110.8 25.6 %collective-permute-start.1 = (bf16[2,512,1024]{2,1,0:T(8,128)(2,1)S(1)}, bf16[2,512,1024]{2,1,0:T(8,128)(2,1)}, u32[]{:S(2)}, u32[]{:S(2)}) collective-permute-start(bf16[2,512,1024]{2,1,0:T(8,128)(2,1)S(1)} %collective-permute-done), channel_id=1, source_target_pairs={{0,1},{1,2},{2,3},{3,0},{4,5},{5,6},{6,7},{7,4},{8,9},{9,10},{10,1... | collective-permute-start | bytes 6291464 | tf_op jit(solution)/shard_map/ppermute | solution.py:29
  136.4 42.6 %collective-permute-start.2 = (bf16[2,512,1024]{2,1,0:T(8,128)(2,1)}, bf16[2,512,1024]{2,1,0:T(8,128)(2,1)}, u32[]{:S(2)}, u32[]{:S(2)}) collective-permute-start(bf16[2,512,1024]{2,1,0:T(8,128)(2,1)} %collective-permute-done.1), channel_id=1, source_target_pairs={{0,1},{1,2},{2,3},{3,0},{4,5},{5,6},{6,7},{7,4},{8,9},{9,10},{10,1... | collective-permute-start | bytes 6291464 | tf_op jit(solution)/shard_map/ppermute | solution.py:29
  136.4 30.8 %copy-start.5 = (f32[1,4096]{1,0:T(1,128)S(1)}, f32[1,4096]{1,0:T(1,128)}, u32[]{:S(2)}) copy-start(f32[1,4096]{1,0:T(1,128)} %param.8) | copy-start | bytes 49156
  177.4 9.5 %copy-start = (bf16[2,512,1024]{2,1,0:T(8,128)(2,1)S(1)}, bf16[2,512,1024]{2,1,0:T(8,128)(2,1)}, u32[]{:S(2)}) copy-start(bf16[2,512,1024]{2,1,0:T(8,128)(2,1)} %all-gather.4.cloned.1.call-done) | copy-start | bytes 6291460
  179.0 6.4 %copy-start.2 = (bf16[2,512,1024]{2,1,0:T(8,128)(2,1)S(1)}, bf16[2,512,1024]{2,1,0:T(8,128)(2,1)}, u32[]{:S(2)}) copy-start(bf16[2,512,1024]{2,1,0:T(8,128)(2,1)} %copy-done.1) | copy-start | bytes 6291460
  179.0 18.7 %slice-start = ((s8[16777216]{0:T(1024)(128)(4,1)}), s8[4194304]{0:T(1024)(128)(4,1)S(1)}, s32[]{:S(2)}) async-start(s8[16777216]{0:T(1024)(128)(4,1)} %bitcast.38), calls=%async_computation.4 | async-start | bytes 8388608
  185.4 12.3 %slice-start.1 = ((s8[16777216]{0:T(1024)(128)(4,1)}), s8[4194304]{0:T(1024)(128)(4,1)S(1)}, s32[]{:S(2)}) async-start(s8[16777216]{0:T(1024)(128)(4,1)} %bitcast.38), calls=%async_computation.5 | async-start | bytes 8388608
  188.3 9.4 %slice-start.2 = ((s8[16777216]{0:T(1024)(128)(4,1)}), s8[4194304]{0:T(1024)(128)(4,1)S(1)}, s32[]{:S(2)}) async-start(s8[16777216]{0:T(1024)(128)(4,1)} %bitcast.38), calls=%async_computation.6 | async-start | bytes 8388608
  194.6 3.7 %slice-start.3 = ((s8[16777216]{0:T(1024)(128)(4,1)}), s8[4194304]{0:T(1024)(128)(4,1)S(1)}, s32[]{:S(2)}) async-start(s8[16777216]{0:T(1024)(128)(4,1)} %bitcast.38), calls=%async_computation.7 | async-start | bytes 8388608
  226.4 9.8 %copy-start.4 = (bf16[2,512,1024]{1,2,0:T(8,128)(2,1)S(1)}, bf16[2,512,1024]{1,2,0:T(8,128)(2,1)}, u32[]{:S(2)}) copy-start(bf16[2,512,1024]{1,2,0:T(8,128)(2,1)} %copy.11) | copy-start | bytes 6291460
  253.6 70.3 %copy-start.3 = (bf16[1,2,256,1024]{3,2,1,0:T(8,128)(2,1)S(1)}, bf16[1,2,256,1024]{3,2,1,0:T(8,128)(2,1)}, u32[]{:S(2)}) copy-start(bf16[1,2,256,1024]{3,2,1,0:T(8,128)(2,1)} %param.7) | copy-start | bytes 3145732
Sparse Core Ops, SparseCore 0:
  9.5 51.7 all-gather.3
  62.9 44.3 all-gather.5
  253.8 70.1 reduce-scatter.1
